TPU v7x, 32 devices: a whole 2x2x4 slice. The times are simulated.
32 devices in a mesh: batch: 4 (over x, core), seq: 8 (over z, y).
Axes of the slice: x: 2, y: 2, z: 4, core: 2. Of those that a mesh axis runs over, the one named last changes fastest.
Arguments:
- signal: bfloat16 [4, 2048, 256], P('batch', 'seq'), may hold values from -0.3125 to 0.3125
- grad_out: bfloat16 [4, 2048, 256], P('batch', 'seq'), may hold values from -6 to 6
- filter_taps: float32 [2048, 256], P('seq'), may hold values from -0.3125 to 0.3125
- skip_gain: float32 [256], replicated, may hold values from 0.5 to 2
Outputs:
- input_grad: bfloat16 [4, 2048, 256], P('batch', 'seq')
- filter_grad: float32 [2048, 256], P('seq')
All inputs are finite; a program needn't handle non-finite values.
Results may differ from a plain program's by a relative error of at most 0.001.
Values sent between devices are 32-bit elements; how exact they have to be, the bound alone decides.
A program may use at most 64 MiB of HBM per device.

v0:
```python
import jax
import jax.numpy as jnp
from jax import lax
from jax.sharding import PartitionSpec as P


def angle_table(height, width, period):
    product = lax.broadcasted_iota(jnp.int32, (height, width), 0) * lax.broadcasted_iota(
        jnp.int32, (height, width), 1
    )
    return 2.0 * jnp.pi / period * (product % period).astype(jnp.float32)


def angle_of(product, period):
    return 2.0 * jnp.pi / period * (product % period).astype(jnp.float32)


def coarse_order(slot, seq_count):
    pair_index = slot // 2
    odd_slot = slot % 2
    return jnp.where(
        pair_index == 0,
        odd_slot * seq_count,
        jnp.where(odd_slot == 0, pair_index, 2 * seq_count - pair_index),
    )


def contract(form, table, operand):
    return jnp.einsum(form, table, operand, precision=lax.Precision.HIGHEST)


def forward_spectra(columns):
    seq_count = lax.axis_size("seq")
    row_count = columns.shape[0]
    part_rows = row_count // seq_count
    period_len = 2 * row_count * seq_count
    spread = lax.all_to_all(
        columns.reshape(1, row_count, columns.shape[1]),
        "seq",
        split_axis=1,
        concat_axis=0,
        tiled=True,
    )
    slot_grid = lax.broadcasted_iota(jnp.int32, (2 * seq_count, seq_count), 0)
    source_grid = lax.broadcasted_iota(jnp.int32, (2 * seq_count, seq_count), 1)
    first_table = angle_of(coarse_order(slot_grid, seq_count) * source_grid, 2 * seq_count)
    cos_first = jnp.cos(first_table)
    sin_first = jnp.sin(first_table)
    half_width = spread.shape[2] // 2
    real_in = spread[:, :, :half_width]
    imag_in = spread[:, :, half_width:]
    real_part = contract("ks,srw->krw", cos_first, real_in) + contract(
        "ks,srw->krw", sin_first, imag_in
    )
    imag_part = contract("ks,srw->krw", cos_first, imag_in) - contract(
        "ks,srw->krw", sin_first, real_in
    )
    global_row = lax.axis_index("seq") * part_rows + lax.broadcasted_iota(
        jnp.int32, (2 * seq_count, part_rows), 1
    )
    coarse = coarse_order(lax.broadcasted_iota(jnp.int32, (2 * seq_count, part_rows), 0), seq_count)
    phases = angle_of(global_row * coarse, period_len)
    cos_turn = jnp.cos(phases)[:, :, None]
    sin_turn = jnp.sin(phases)[:, :, None]
    rotated = jnp.stack(
        [real_part * cos_turn + imag_part * sin_turn, imag_part * cos_turn - real_part * sin_turn]
    )
    inner_table = angle_table(row_count, row_count, row_count)
    cos_inner = jnp.cos(inner_table)
    sin_inner = jnp.sin(inner_table)
    pieces = lax.all_to_all(rotated, "seq", split_axis=1, concat_axis=2, tiled=True)
    real_sum = contract("qr,krw->kqw", cos_inner, pieces[0]) + contract(
        "qr,krw->kqw", sin_inner, pieces[1]
    )
    imag_sum = contract("qr,krw->kqw", cos_inner, pieces[1]) - contract(
        "qr,krw->kqw", sin_inner, pieces[0]
    )
    return jnp.stack([real_sum, imag_sum])


def split_pairs(packed):
    reversed_q = packed[:, :, ::-1]
    zero_row = jnp.roll(reversed_q[:, 0], 1, axis=1)
    own_pair = jnp.stack([zero_row, reversed_q[:, 1]], axis=1)
    partner = jnp.where(lax.axis_index("seq") == 0, own_pair, reversed_q[:, ::-1])
    first = jnp.stack([0.5 * (packed[0] + partner[0]), 0.5 * (packed[1] - partner[1])])
    second = jnp.stack([0.5 * (packed[1] + partner[1]), 0.5 * (partner[0] - packed[0])])
    return (first, second)


def inverse_rows(spectra):
    seq_count = lax.axis_size("seq")
    row_count = spectra.shape[2]
    period_len = 2 * row_count * seq_count
    inner_table = angle_table(row_count, row_count, row_count)
    cos_inner = jnp.cos(inner_table)
    sin_inner = jnp.sin(inner_table)
    real_sum = contract("qr,krw->kqw", cos_inner, spectra[0]) - contract(
        "qr,krw->kqw", sin_inner, spectra[1]
    )
    imag_sum = contract("qr,krw->kqw", cos_inner, spectra[1]) + contract(
        "qr,krw->kqw", sin_inner, spectra[0]
    )
    coarse = coarse_order(
        2 * lax.axis_index("seq") + lax.broadcasted_iota(jnp.int32, (2, row_count), 0), seq_count
    )
    position = lax.broadcasted_iota(jnp.int32, (2, row_count), 1)
    phases = angle_of(position * coarse, period_len)
    cos_turn = jnp.cos(phases)[:, :, None]
    sin_turn = jnp.sin(phases)[:, :, None]
    rotated = jnp.stack(
        [real_sum * cos_turn - imag_sum * sin_turn, real_sum * sin_turn + imag_sum * cos_turn]
    )
    target_grid = lax.broadcasted_iota(jnp.int32, (seq_count, 2 * seq_count), 0)
    slot_grid = lax.broadcasted_iota(jnp.int32, (seq_count, 2 * seq_count), 1)
    last_table = angle_of(target_grid * coarse_order(slot_grid, seq_count), 2 * seq_count)
    cos_last = jnp.cos(last_table)
    sin_last = jnp.sin(last_table)
    pieces = lax.all_to_all(rotated, "seq", split_axis=2, concat_axis=1, tiled=True)
    value = contract("sk,krw->srw", cos_last, pieces[0]) - contract(
        "sk,krw->srw", sin_last, pieces[1]
    )
    other = contract("sk,krw->srw", sin_last, pieces[0]) + contract(
        "sk,krw->srw", cos_last, pieces[1]
    )
    gathered = (value / period_len, other / period_len)
    gathered = jnp.concatenate([gathered[0], gathered[1]], axis=2)
    home_rows = lax.all_to_all(gathered, "seq", split_axis=0, concat_axis=1, tiled=True)
    return home_rows.reshape(row_count, home_rows.shape[2])


def invert_all(spectra):
    half_width = spectra.shape[3] // 2
    joined = jnp.stack(
        [
            spectra[0, :, :, :half_width] - spectra[1, :, :, half_width:],
            spectra[1, :, :, :half_width] + spectra[0, :, :, half_width:],
        ]
    )
    return inverse_rows(joined)


def shards(signal, grad_out, filter_taps, skip_gain):
    channels = filter_taps.shape[1]
    signal_rows = signal[0].astype(jnp.float32)
    grad_rows = grad_out[0].astype(jnp.float32)
    tap_half = filter_taps.shape[1] // 2
    columns = jnp.concatenate(
        [signal_rows, filter_taps[:, :tap_half], grad_rows, filter_taps[:, tap_half:]], axis=1
    )
    first, second = split_pairs(forward_spectra(columns))
    signal_spec = first[:, :, :, :channels]
    grad_spec = second[:, :, :, :channels]
    own_spec = jnp.concatenate([first[:, :, :, channels:], second[:, :, :, channels:]], axis=3)
    input_spec = jnp.stack(
        [
            grad_spec[0] * own_spec[0] + grad_spec[1] * own_spec[1],
            grad_spec[1] * own_spec[0] - grad_spec[0] * own_spec[1],
        ]
    )
    filter_terms = jnp.stack(
        [
            grad_spec[0] * signal_spec[0] + grad_spec[1] * signal_spec[1],
            grad_spec[1] * signal_spec[0] - grad_spec[0] * signal_spec[1],
        ]
    )
    summed = lax.psum(filter_terms, "batch")
    rows_back = invert_all(jnp.concatenate([input_spec, summed], axis=3))
    filter_grad = rows_back[:, channels:]
    input_grad = (rows_back[:, :channels] + skip_gain[None, :] * grad_rows).astype(jnp.bfloat16)
    return (input_grad[None], filter_grad)


def solution(mesh):
    return jax.shard_map(
        shards,
        mesh=mesh,
        in_specs=(P("batch", "seq", None), P("batch", "seq", None), P("seq", None), P()),
        out_specs=(P("batch", "seq", None), P("seq", None)),
        check_vma=False,
    )
```

profile of v0, /device:TPU:0, one launch (start us, length us, event | category | flops | bytes accessed | tf_op | source)
XLA Modules:
  0.0 231.8 jit_solution(8577959397815715858)
XLA Ops:
  9.2 1.7 copy.37
  10.9 7.3 %all-to-all-start = ((f32[1,256,768]{2,0,1:T(1,128)}), f32[1,256,768]{2,0,1:T(1,128)S(1)}, u32[]{:S(2)}, u32[]{:S(2)}) async-start(f32[1,256,768]{2,0,1:T(1,128)} %copy.37), calls=%async_computation | async-start | bytes 1572864 | tf_op jit(solution)/shard_map/all_to_all | solution.py:37
  18.4 20.0 %all-to-all-done = f32[1,256,768]{2,0,1:T(1,128)S(1)} async-done(((f32[1,256,768]{2,0,1:T(1,128)}), f32[1,256,768]{2,0,1:T(1,128)S(1)}, u32[]{:S(2)}, u32[]{:S(2)}) %all-to-all-start) | async-done | bytes 786464 | tf_op jit(solution)/shard_map/all_to_all | solution.py:37
  42.7 1.7 copy.40
  44.4 3.6 %all-to-all-start.1 = ((f32[2,16,32,384]{3,2,0,1:T(8,128)}), f32[2,16,32,384]{3,2,0,1:T(8,128)S(1)}, u32[]{:S(2)}, u32[]{:S(2)}) async-start(f32[2,16,32,384]{3,2,0,1:T(8,128)} %copy.40), calls=%async_computation.1 | async-start | bytes 3145728 | tf_op jit(solution)/shard_map/all_to_all | solution.py:71
  48.2 36.9 %all-to-all-done.1 = f32[2,16,32,384]{3,2,0,1:T(8,128)S(1)} async-done(((f32[2,16,32,384]{3,2,0,1:T(8,128)}), f32[2,16,32,384]{3,2,0,1:T(8,128)S(1)}, u32[]{:S(2)}, u32[]{:S(2)}) %all-to-all-start.1) | async-done | bytes 1572896 | tf_op jit(solution)/shard_map/all_to_all | solution.py:71
  85.5 2.2 fusion.36
  87.7 2.2 fusion.34
  89.9 2.2 convolution_subtract_fusion
  92.1 2.2 convolution_add_fusion
  94.3 1.3 pad_maximum_fusion
  95.6 1.3 fusion.4
  96.9 11.2 %rev.4 = f32[2,2,256,384]{2,3,1,0:T(8,128)S(1)} reverse(f32[2,2,256,384]{2,3,1,0:T(8,128)} %pad_maximum_fusion), dimensions={1,2} | reverse | bytes 3145728 | tf_op jit(solution)/shard_map/rev | solution.py:85
  108.1 7.2 %slice.127 = f32[2,1,256,384]{2,3,1,0:T(8,128)} reverse(f32[2,1,256,384]{2,3,1,0:T(8,128)} %get-tuple-element.17), dimensions={2} | reverse | bytes 1572864 | tf_op jit(solution)/shard_map/slice | solution.py:84
  115.3 7.2 %slice.123 = f32[2,1,256,384]{2,3,0,1:T(8,128)} reverse(f32[2,1,256,384]{2,3,0,1:T(8,128)} %get-tuple-element.16), dimensions={2} | reverse | bytes 1572864 | tf_op jit(solution)/shard_map/slice | solution.py:83
  123.8 1.4 maximum_bitcast_fusion.1
  129.7 33.8 %all-reduce.2.cloned.1.call-done = f32[2,2,256,256]{2,3,1,0:T(8,128)} async-done(((f32[2,2,256,256]{2,3,1,0:T(8,128)}), f32[2,2,256,256]{2,3,1,0:T(8,128)}) %all-reduce.2.cloned.1.call-update) | async-done | bytes 1048592 | tf_op jit(solution)/shard_map/psum | solution.py:167
  163.5 1.7 fusion.15
  165.2 1.6 fusion.30
  166.7 1.6 fusion.32
  168.3 1.6 convolution_add_fusion.2
  169.9 1.6 subtract_bitcast_fusion.1
  172.2 30.5 %all_to_all.51 = f32[2,2,256,256]{3,1,0,2:T(2,128)S(1)} all-to-all(f32[2,2,256,256]{3,1,0,2:T(2,128)S(1)} %copy.49), channel_id=1, replica_groups=mesh['batch'=4,'seq'=8] {'seq'}, dimensions={2} | all-to-all | bytes 2097152 | tf_op jit(solution)/shard_map/all_to_all | solution.py:119
  206.7 17.4 %all_to_all.52 = f32[8,32,512]{2,1,0:T(8,128)S(1)} all-to-all(f32[8,32,512]{2,1,0:T(8,128)S(1)} %copy.53), channel_id=1, replica_groups=mesh['batch'=4,'seq'=8] {'seq'}, dimensions={0} | all-to-all | bytes 1048576 | tf_op jit(solution)/shard_map/all_to_all | solution.py:128
  (61 shorter events, 18.1 us)
Async XLA Ops:
  10.9 27.5 %all-to-all-start = ((f32[1,256,768]{2,0,1:T(1,128)}), f32[1,256,768]{2,0,1:T(1,128)S(1)}, u32[]{:S(2)}, u32[]{:S(2)}) async-start(f32[1,256,768]{2,0,1:T(1,128)} %copy.37), calls=%async_computation | async-start | bytes 1572864 | tf_op jit(solution)/shard_map/all_to_all | solution.py:37
  44.4 40.8 %all-to-all-start.1 = ((f32[2,16,32,384]{3,2,0,1:T(8,128)}), f32[2,16,32,384]{3,2,0,1:T(8,128)S(1)}, u32[]{:S(2)}, u32[]{:S(2)}) async-start(f32[2,16,32,384]{3,2,0,1:T(8,128)} %copy.40), calls=%async_computation.1 | async-start | bytes 3145728 | tf_op jit(solution)/shard_map/all_to_all | solution.py:71
  48.0 115.5 %all-reduce.2.cloned.1.call-start = ((), (), s32[]{:S(2)}) async-start(), calls=%async_computation.4 | async-start | bytes 2097152 | tf_op jit(solution)/shard_map/psum | solution.py:167
  122.5 2.6 %copy-start.4 = (f32[2,1,256,384]{2,3,1,0:T(8,128)S(1)}, f32[2,1,256,384]{2,3,1,0:T(8,128)}, u32[]{:S(2)}) copy-start(f32[2,1,256,384]{2,3,1,0:T(8,128)} %slice.127) | copy-start | bytes 2359300
  125.8 0.9 copy-start
  125.8 1.1 copy-start.2
  126.9 1.5 copy-start.1
  126.9 1.7 copy-start.3
  206.3 17.8 %copy-start.5 = (bf16[1,256,256]{2,1,0:T(8,128)(2,1)S(1)}, bf16[1,256,256]{2,1,0:T(8,128)(2,1)}, u32[]{:S(2)}) copy-start(bf16[1,256,256]{2,1,0:T(8,128)(2,1)} %param.5) | copy-start | bytes 393220
  206.4 17.8 %copy-start.6 = (f32[256]{0:T(256)S(1)}, f32[256]{0:T(256)}, u32[]{:S(2)}) copy-start(f32[256]{0:T(256)} %param.7) | copy-start | bytes 3076
Sparse Core Ops, SparseCore 0:
  128.1 35.3 all-reduce.1
where the time goes:
time: 234 us; the launch traced here: 232 us
  waiting for transfers between devices  90.7 us (39%)
  blocking collectives  48 us (21%)
  local copies, waits for them, and re-layouts  36 us (15%)
  matrix products  20.8 us (9%)
  between operations  14.4 us (6%)
  starting transfers between devices  11.1 us (5%)
  other arithmetic  10.9 us (5%)
    all_to_all x1, waiting for transfers between devices, forward_spectra(): lax.all_to_all(rotated, 'seq', split_axis=1, concat_axis=2, tiled=True)  36.9 us
    psum x1, waiting for transfers between devices, shards(): summed = lax.psum(filter_terms, 'batch')  33.8 us
    all_to_all x1, blocking collectives, inverse_rows(): lax.all_to_all(rotated, 'seq', split_axis=2, concat_axis=1, tiled=True)  30.5 us
    dot_general x16, matrix products, contract(): return jnp.einsum(form, table, operand, precision=lax.Precision.HIGHEST)  20.8 us
    all_to_all x1, waiting for transfers between devices, forward_spectra(): lax.all_to_all(columns.reshape(1, row_count, columns.shape[1]), 'seq', sp...  20 us
    all_to_all x1, blocking collectives, inverse_rows(): lax.all_to_all(gathered, 'seq', split_axis=0, concat_axis=1, tiled=True)  17.4 us
    rev x1, local copies, waits for them, and re-layouts, split_pairs(): reversed_q[:, ::-1]  11.2 us
    slice x2, local copies, waits for them, and re-layouts, split_pairs(): zero_row = jnp.roll(reversed_q[:, 0], 1, axis=1)  8.44 us
  transfers between devices with their start and end apart: 3, of which 3 were waited for; matrix products, arithmetic and copies ran while one was open for 1% of the time, Pallas kernels for 0%

commit v1 on v0

--- a/solution.py
+++ b/solution.py
@@ -68,7 +68,10 @@
     inner_table = angle_table(row_count, row_count, row_count)
     cos_inner = jnp.cos(inner_table)
     sin_inner = jnp.sin(inner_table)
-    pieces = lax.all_to_all(rotated, "seq", split_axis=1, concat_axis=2, tiled=True)
+    count = lax.axis_size("seq")
+    shards_2 = jnp.stack(jnp.split(rotated, count, axis=1), axis=0)
+    shards_2 = lax.all_to_all(shards_2, "seq", split_axis=0, concat_axis=0)
+    pieces = jnp.concatenate(shards_2, axis=2)
     real_sum = contract("qr,krw->kqw", cos_inner, pieces[0]) + contract(
         "qr,krw->kqw", sin_inner, pieces[1]
     )

time: 234 us -> 238 us (1.017)
  other arithmetic: 10.9 us -> 16.8 us
    unnamed x1 -> x8, other arithmetic: 1.25 us -> 6.51 us
where the time goes in v1:
time: 238 us; the launch traced here: 236 us
  waiting for transfers between devices  90.7 us (38%)
  blocking collectives  48 us (20%)
  local copies, waits for them, and re-layouts  35.6 us (15%)
  matrix products  19 us (8%)
  other arithmetic  16.8 us (7%)
  between operations  14.4 us (6%)
  starting transfers between devices  11.1 us (5%)
    all_to_all x1, waiting for transfers between devices, forward_spectra(): shards_2 = lax.all_to_all(shards_2, 'seq', split_axis=0, concat_axis=0)  36.9 us
    psum x1, waiting for transfers between devices, shards(): summed = lax.psum(filter_terms, 'batch')  33.8 us
    all_to_all x1, blocking collectives, inverse_rows(): lax.all_to_all(rotated, 'seq', split_axis=2, concat_axis=1, tiled=True)  30.5 us
    all_to_all x1, waiting for transfers between devices, forward_spectra(): lax.all_to_all(columns.reshape(1, row_count, columns.shape[1]), 'seq', sp...  20 us
    dot_general x16, matrix products, contract(): return jnp.einsum(form, table, operand, precision=lax.Precision.HIGHEST)  19 us
    all_to_all x1, blocking collectives, inverse_rows(): lax.all_to_all(gathered, 'seq', split_axis=0, concat_axis=1, tiled=True)  17.4 us
    rev x1, local copies, waits for them, and re-layouts, split_pairs(): reversed_q[:, ::-1]  11.2 us
    slice x2, local copies, waits for them, and re-layouts, split_pairs(): zero_row = jnp.roll(reversed_q[:, 0], 1, axis=1)  8.44 us
  transfers between devices with their start and end apart: 3, of which 3 were waited for; matrix products, arithmetic and copies ran while one was open for 1% of the time, Pallas kernels for 0%

profile of v1, /device:TPU:0, one launch (start us, length us, event | category | flops | bytes accessed | tf_op | source)
XLA Modules:
  0.0 235.6 jit_solution(18321370509550641613)
XLA Ops:
  9.2 1.7 copy.24
  10.9 7.3 %all-to-all-start = ((f32[1,256,768]{2,0,1:T(1,128)}), f32[1,256,768]{2,0,1:T(1,128)S(1)}, u32[]{:S(2)}, u32[]{:S(2)}) async-start(f32[1,256,768]{2,0,1:T(1,128)} %copy.24), calls=%async_computation | async-start | bytes 1572864 | tf_op jit(solution)/shard_map/all_to_all | solution.py:37
  18.4 20.0 %all-to-all-done = f32[1,256,768]{2,0,1:T(1,128)S(1)} async-done(((f32[1,256,768]{2,0,1:T(1,128)}), f32[1,256,768]{2,0,1:T(1,128)S(1)}, u32[]{:S(2)}, u32[]{:S(2)}) %all-to-all-start) | async-done | bytes 786464 | tf_op jit(solution)/shard_map/all_to_all | solution.py:37
  48.6 3.6 %all-to-all-start.1 = ((f32[8,2,2,32,384]{4,2,3,1,0:T(2,128)}), f32[8,2,2,32,384]{4,2,3,1,0:T(2,128)S(1)}, u32[]{:S(2)}, u32[]{:S(2)}) async-start(f32[8,2,2,32,384]{4,2,3,1,0:T(2,128)} %fusion.63), calls=%async_computation.1 | async-start | bytes 3145728 | tf_op jit(solution)/shard_map/all_to_all | solution.py:73
  52.5 36.9 %all-to-all-done.1 = f32[8,2,2,32,384]{4,2,3,1,0:T(2,128)S(1)} async-done(((f32[8,2,2,32,384]{4,2,3,1,0:T(2,128)}), f32[8,2,2,32,384]{4,2,3,1,0:T(2,128)S(1)}, u32[]{:S(2)}, u32[]{:S(2)}) %all-to-all-start.1) | async-done | bytes 1572896 | tf_op jit(solution)/shard_map/all_to_all | solution.py:73
  90.6 1.8 fusion.36
  92.8 1.8 fusion.34
  94.6 1.8 convolution_subtract_fusion
  96.4 1.8 convolution_add_fusion
  98.1 1.3 pad_maximum_fusion
  99.4 1.3 fusion.4
  100.7 11.2 %rev.4 = f32[2,2,256,384]{2,3,1,0:T(8,128)S(1)} reverse(f32[2,2,256,384]{2,3,1,0:T(8,128)} %pad_maximum_fusion), dimensions={1,2} | reverse | bytes 3145728 | tf_op jit(solution)/shard_map/rev | solution.py:88
  111.9 7.2 %slice.127 = f32[2,1,256,384]{2,3,1,0:T(8,128)} reverse(f32[2,1,256,384]{2,3,1,0:T(8,128)} %get-tuple-element.17), dimensions={2} | reverse | bytes 1572864 | tf_op jit(solution)/shard_map/slice | solution.py:87
  119.1 7.2 %slice.123 = f32[2,1,256,384]{2,3,0,1:T(8,128)} reverse(f32[2,1,256,384]{2,3,0,1:T(8,128)} %get-tuple-element.16), dimensions={2} | reverse | bytes 1572864 | tf_op jit(solution)/shard_map/slice | solution.py:86
  126.3 1.2 slice.150
  127.6 1.4 maximum_bitcast_fusion.1
  133.5 33.8 %all-reduce.2.cloned.1.call-done = f32[2,2,256,256]{2,3,1,0:T(8,128)} async-done(((f32[2,2,256,256]{2,3,1,0:T(8,128)}), f32[2,2,256,256]{2,3,1,0:T(8,128)}) %all-reduce.2.cloned.1.call-update) | async-done | bytes 1048592 | tf_op jit(solution)/shard_map/psum | solution.py:170
  167.3 1.7 fusion.15
  169.0 1.6 fusion.30
  170.5 1.6 fusion.32
  172.1 1.6 convolution_add_fusion.2
  173.7 1.6 subtract_bitcast_fusion.1
  176.0 30.5 %all_to_all.41 = f32[2,2,256,256]{3,1,0,2:T(2,128)S(1)} all-to-all(f32[2,2,256,256]{3,1,0,2:T(2,128)S(1)} %copy.32), channel_id=1, replica_groups=mesh['batch'=4,'seq'=8] {'seq'}, dimensions={2} | all-to-all | bytes 2097152 | tf_op jit(solution)/shard_map/all_to_all | solution.py:122
  210.5 17.4 %all_to_all.42 = f32[8,32,512]{2,1,0:T(8,128)S(1)} all-to-all(f32[8,32,512]{2,1,0:T(8,128)S(1)} %copy.36), channel_id=1, replica_groups=mesh['batch'=4,'seq'=8] {'seq'}, dimensions={0} | all-to-all | bytes 1048576 | tf_op jit(solution)/shard_map/all_to_all | solution.py:131
  (66 shorter events, 24.1 us)
Async XLA Ops:
  10.9 27.5 %all-to-all-start = ((f32[1,256,768]{2,0,1:T(1,128)}), f32[1,256,768]{2,0,1:T(1,128)S(1)}, u32[]{:S(2)}, u32[]{:S(2)}) async-start(f32[1,256,768]{2,0,1:T(1,128)} %copy.24), calls=%async_computation | async-start | bytes 1572864 | tf_op jit(solution)/shard_map/all_to_all | solution.py:37
  48.6 40.8 %all-to-all-start.1 = ((f32[8,2,2,32,384]{4,2,3,1,0:T(2,128)}), f32[8,2,2,32,384]{4,2,3,1,0:T(2,128)S(1)}, u32[]{:S(2)}, u32[]{:S(2)}) async-start(f32[8,2,2,32,384]{4,2,3,1,0:T(2,128)} %fusion.63), calls=%async_computation.1 | async-start | bytes 3145728 | tf_op jit(solution)/shard_map/all_to_all | solution.py:73
  52.2 115.1 %all-reduce.2.cloned.1.call-start = ((), (), s32[]{:S(2)}) async-start(), calls=%async_computation.4 | async-start | bytes 2097152 | tf_op jit(solution)/shard_map/psum | solution.py:170
  126.3 2.6 %copy-start.4 = (f32[2,1,256,384]{2,3,1,0:T(8,128)S(1)}, f32[2,1,256,384]{2,3,1,0:T(8,128)}, u32[]{:S(2)}) copy-start(f32[2,1,256,384]{2,3,1,0:T(8,128)} %slice.127) | copy-start | bytes 2359300
  129.5 0.9 copy-start
  129.6 1.1 copy-start.2
  130.7 1.5 copy-start.1
  130.7 1.7 copy-start.3
  210.1 17.8 %copy-start.5 = (bf16[1,256,256]{2,1,0:T(8,128)(2,1)S(1)}, bf16[1,256,256]{2,1,0:T(8,128)(2,1)}, u32[]{:S(2)}) copy-start(bf16[1,256,256]{2,1,0:T(8,128)(2,1)} %param.5) | copy-start | bytes 393220
  210.2 17.8 %copy-start.6 = (f32[256]{0:T(256)S(1)}, f32[256]{0:T(256)}, u32[]{:S(2)}) copy-start(f32[256]{0:T(256)} %param.7) | copy-start | bytes 3076
Sparse Core Ops, SparseCore 0:
  131.9 35.3 all-reduce.1
